TPU v7x, 32 devices: a whole 2x2x4 slice. The times are simulated.
32 devices in a mesh: bank: 4 (over z), zero: 8 (over y, x, core).
Axes of the slice: x: 2, y: 2, z: 4, core: 2. Of those that a mesh axis runs over, the one named last changes fastest.
Arguments:
- w_gate: float32 [128, 2048, 768], P('bank', 'zero'), may hold values from -0.1875 to 0.1875
- w_up: float32 [128, 2048, 768], P('bank', 'zero'), may hold values from -0.1875 to 0.1875
- router_weight: float32 [2048, 128], P('zero', 'bank'), may hold values from -0.125 to 0.125
- router_gain: float32 [2048], P('zero'), may hold values from 0.25 to 1.75
Outputs:
- serve_gate: bfloat16 [128, 2048, 768], P('bank', None, 'zero')
- serve_up: bfloat16 [128, 2048, 768], P('bank', None, 'zero')
- scale_gate: float32 [128, 768], P('bank', 'zero')
- scale_up: float32 [128, 768], P('bank', 'zero')
- serve_router: bfloat16 [2048, 128], replicated
All inputs are finite; a program needn't handle non-finite values.
Results may differ from a plain program's by a relative error of at most 0.001.
Values may be sent and summed in bfloat16 or wider, within the bound.
A program may use at most 192 MiB of HBM per device.

v0:
```python
import jax
import jax.numpy as jnp
from jax import lax
from jax.sharding import PartitionSpec as P


def shards(w_gate, w_up, router_weight, router_gain):
    total_gate, total_up = lax.psum(
        (jnp.sum(w_gate * w_gate, axis=1), jnp.sum(w_up * w_up, axis=1)), "zero"
    )
    scale_gate = jnp.sqrt(total_gate)
    scale_up = jnp.sqrt(total_up)
    narrow_gate, narrow_up = (
        (w_gate / jnp.expand_dims(scale_gate, 1)).astype(jnp.bfloat16),
        (w_up / jnp.expand_dims(scale_up, 1)).astype(jnp.bfloat16),
    )
    serve_gate, serve_up = (
        lax.all_to_all(narrow_gate, "zero", split_axis=2, concat_axis=1, tiled=True),
        lax.all_to_all(narrow_up, "zero", split_axis=2, concat_axis=1, tiled=True),
    )
    scale_gate = lax.dynamic_slice_in_dim(
        scale_gate, lax.axis_index("zero") * serve_gate.shape[2], serve_gate.shape[2], axis=1
    )
    scale_up = lax.dynamic_slice_in_dim(
        scale_up, lax.axis_index("zero") * serve_up.shape[2], serve_up.shape[2], axis=1
    )
    part_router = (router_weight * router_gain[:, None]).astype(jnp.bfloat16)
    row_router = lax.all_gather(part_router, "zero", axis=0, tiled=True)
    serve_router = lax.all_gather(row_router, "bank", axis=1, tiled=True)
    return (serve_gate, serve_up, scale_gate, scale_up, serve_router)


def solution(mesh):
    placed = (P("bank", "zero", None), P("bank", "zero", None), P("zero", "bank"), P("zero"))
    return jax.shard_map(
        shards,
        mesh=mesh,
        in_specs=placed,
        out_specs=(
            P("bank", None, "zero"),
            P("bank", None, "zero"),
            P("bank", "zero"),
            P("bank", "zero"),
            P(),
        ),
        check_vma=False,
    )
```

profile of v0, /device:TPU:0, one launch (start us, length us, event | category | flops | bytes accessed | tf_op | source)
XLA Modules:
  0.0 481.0 jit_solution(10650282860068963028)
XLA Ops:
  7.2 0.0 all-reduce.3.cloned.1.call-start
  7.2 17.3 %multiply_reduce_fusion = (f32[32,768]{1,0:T(8,128)}, f32[32,768]{1,0:T(8,128)}) fusion(f32[32,256,768]{2,1,0:T(8,128)} %param.5, f32[32,256,768]{2,1,0:T(8,128)} %param.4), kind=kLoop, calls=%fused_computation.1 | loop fusion | flops 25116672 | bytes 50528256 | tf_op jit(solution)/shard_map/reduce_sum | solution.py:9
  24.5 0.0 all-reduce.3.cloned.1.call-update
  24.5 25.1 %copy.25 = f32[32,256,768]{1,0,2:T(8,128)} copy(f32[32,256,768]{2,1,0:T(8,128)} %param.5) | data formatting | bytes 50331648 | tf_op args[1]
  49.6 31.5 %all-reduce.3.cloned.1.call-done = (f32[32,768]{1,0:T(8,128)}, f32[32,768]{1,0:T(8,128)}) async-done(((f32[32,768]{1,0:T(8,128)}, f32[32,768]{1,0:T(8,128)}), (f32[32,768]{1,0:T(8,128)}, f32[32,768]{1,0:T(8,128)})) %all-reduce.3.cloned.1.call-update) | async-done | bytes 196624 | tf_op jit(solution)/shard_map/psum | solution.py:8
  81.1 0.9 sqrt.7
  82.1 0.2 copy.24
  82.2 14.1 %divide_convert_fusion = bf16[32,256,768]{1,0,2:T(8,128)(2,1)} fusion(f32[32,256,768]{1,0,2:T(8,128)} %copy.25, f32[32,768]{0,1:T(8,128)S(1)} %copy.24), kind=kLoop, calls=%fused_computation | loop fusion | flops 12582912 | bytes 37847040 | tf_op jit(solution)/shard_map/convert_element_type | solution.py:15
  96.4 5.4 %all-to-all-start.1 = ((bf16[32,256,768]{1,0,2:T(8,128)(2,1)}), bf16[32,256,768]{1,0,2:T(8,128)(2,1)}, u32[]{:S(2)}, u32[]{:S(2)}) async-start(bf16[32,256,768]{1,0,2:T(8,128)(2,1)} %divide_convert_fusion), calls=%async_computation.1 | async-start | bytes 25165824 | tf_op jit(solution)/shard_map/all_to_all | solution.py:19
  101.8 25.1 %copy.21 = f32[32,256,768]{1,0,2:T(8,128)} copy(f32[32,256,768]{2,1,0:T(8,128)} %param.4) | data formatting | bytes 50331648 | tf_op args[0]
  126.9 0.2 copy.20
  127.1 0.0 copy-start.1
  127.1 14.1 %divide_convert_fusion.1 = bf16[32,256,768]{1,0,2:T(8,128)(2,1)} fusion(f32[32,256,768]{1,0,2:T(8,128)} %copy.21, f32[32,768]{0,1:T(8,128)S(1)} %copy.20), kind=kLoop, calls=%fused_computation.2 | loop fusion | flops 12582912 | bytes 37847040 | tf_op jit(solution)/shard_map/convert_element_type | solution.py:14
  141.3 99.5 %all-to-all-done.1 = bf16[32,256,768]{1,0,2:T(8,128)(2,1)} async-done(((bf16[32,256,768]{1,0,2:T(8,128)(2,1)}), bf16[32,256,768]{1,0,2:T(8,128)(2,1)}, u32[]{:S(2)}, u32[]{:S(2)}) %all-to-all-start.1) | async-done | bytes 12582944 | tf_op jit(solution)/shard_map/all_to_all | solution.py:19
  240.8 5.4 %all-to-all-start = ((bf16[32,256,768]{1,0,2:T(8,128)(2,1)}), bf16[32,256,768]{1,0,2:T(8,128)(2,1)}, u32[]{:S(2)}, u32[]{:S(2)}) async-start(bf16[32,256,768]{1,0,2:T(8,128)(2,1)} %divide_convert_fusion.1), calls=%async_computation | async-start | bytes 25165824 | tf_op jit(solution)/shard_map/all_to_all | solution.py:18
  246.2 142.4 %all_gather.6 = bf16[2048,32]{0,1:T(8,128)(2,1)S(1)} all-gather(bf16[256,32]{0,1:T(8,128)(2,1)S(1)} %multiply_convert_fusion), channel_id=1, replica_groups=mesh['bank'=4,'zero'=8] {'zero'}, dimensions={0}, use_global_device_ids=true | all-gather | bytes 147456 | tf_op jit(solution)/shard_map/all_gather | solution.py:28
  388.6 16.1 %all_gather.7 = bf16[2048,128]{0,1:T(8,128)(2,1)S(1)} all-gather(bf16[2048,32]{0,1:T(8,128)(2,1)S(1)} %all_gather.6), channel_id=1, replica_groups=mesh['bank'=4,'zero'=8] {'bank'}, dimensions={1}, use_global_device_ids=true | all-gather | bytes 655360 | tf_op jit(solution)/shard_map/all_gather | solution.py:29
  404.6 1.0 copy.28
  405.6 0.7 constant_dynamic-slice_fusion
  406.3 0.7 constant_dynamic-slice_fusion.1
  407.0 14.1 %copy.27 = bf16[32,8,256,96]{2,1,3,0:T(8,128)(2,1)} copy(bf16[32,8,256,96]{2,0,3,1:T(8,128)(2,1)} %bitcast.5) | data formatting | bytes 25165824 | tf_op jit(solution)/shard_map/all_to_all | solution.py:19
  421.1 19.5 %all_to_all.33 = bf16[32,2048,96]{1,2,0:T(8,128)(2,1)} reshape(bf16[32,8,256,96]{2,1,3,0:T(8,128)(2,1)} %copy.27) | data formatting | bytes 25165824 | tf_op jit(solution)/shard_map/all_to_all | solution.py:19
  440.6 14.1 %copy.23 = bf16[32,8,256,96]{2,1,3,0:T(8,128)(2,1)} copy(bf16[32,8,256,96]{2,0,3,1:T(8,128)(2,1)} %bitcast.2) | data formatting | bytes 25165824 | tf_op jit(solution)/shard_map/all_to_all | solution.py:18
  454.7 19.5 %all_to_all.29 = bf16[32,2048,96]{1,2,0:T(8,128)(2,1)} reshape(bf16[32,8,256,96]{2,1,3,0:T(8,128)(2,1)} %copy.23) | data formatting | bytes 25165824 | tf_op jit(solution)/shard_map/all_to_all | solution.py:18
  (8 shorter events, 0.0 us)
Async XLA Ops:
  7.2 74.0 %all-reduce.3.cloned.1.call-start = ((), (), s32[]{:S(2)}) async-start(), calls=%async_computation.2 | async-start | bytes 393216 | tf_op jit(solution)/shard_map/psum | solution.py:8
  96.4 144.4 %all-to-all-start.1 = ((bf16[32,256,768]{1,0,2:T(8,128)(2,1)}), bf16[32,256,768]{1,0,2:T(8,128)(2,1)}, u32[]{:S(2)}, u32[]{:S(2)}) async-start(bf16[32,256,768]{1,0,2:T(8,128)(2,1)} %divide_convert_fusion), calls=%async_computation.1 | async-start | bytes 25165824 | tf_op jit(solution)/shard_map/all_to_all | solution.py:19
  101.8 25.1 %copy-start = (f32[32,768]{1,0:T(8,128)S(1)}, f32[32,768]{1,0:T(8,128)}, u32[]{:S(2)}) copy-start(f32[32,768]{1,0:T(8,128)} %get-tuple-element.10) | copy-start | bytes 294916
  127.1 119.0 %copy-start.1 = (f32[256,32]{0,1:T(8,128)S(1)}, f32[256,32]{0,1:T(8,128)}, u32[]{:S(2)}) copy-start(f32[256,32]{0,1:T(8,128)} %param.6) | copy-start | bytes 98308
  127.1 119.0 %copy-start.2 = (f32[256]{0:T(256)S(1)}, f32[256]{0:T(256)}, u32[]{:S(2)}) copy-start(f32[256]{0:T(256)} %param.7) | copy-start | bytes 3076
  240.8 199.8 %all-to-all-start = ((bf16[32,256,768]{1,0,2:T(8,128)(2,1)}), bf16[32,256,768]{1,0,2:T(8,128)(2,1)}, u32[]{:S(2)}, u32[]{:S(2)}) async-start(bf16[32,256,768]{1,0,2:T(8,128)(2,1)} %divide_convert_fusion.1), calls=%async_computation | async-start | bytes 25165824 | tf_op jit(solution)/shard_map/all_to_all | solution.py:18
Sparse Core Ops, SparseCore 0:
  24.6 56.4 all-reduce.2
where the time goes:
time: 483 us; the launch traced here: 481 us
  blocking collectives  158 us (33%)
  waiting for transfers between devices  131 us (27%)
  local copies, waits for them, and re-layouts  121 us (25%)
  other arithmetic  45.5 us (9%)
  between operations  14.1 us (3%)
  starting transfers between devices  10.8 us (2%)
    all_gather x1, blocking collectives, shards(): row_router = lax.all_gather(part_router, 'zero', axis=0, tiled=True)  142 us
    all_to_all x1, waiting for transfers between devices, shards(): lax.all_to_all(narrow_up, 'zero', split_axis=2, concat_axis=1, tiled=True)  99.5 us
    unnamed x9, local copies, waits for them, and re-layouts  51.3 us
    all_to_all x2, local copies, waits for them, and re-layouts, shards(): lax.all_to_all(narrow_gate, 'zero', split_axis=2, concat_axis=1, tiled=True)  33.6 us
    all_to_all x2, local copies, waits for them, and re-layouts, shards(): lax.all_to_all(narrow_up, 'zero', split_axis=2, concat_axis=1, tiled=True)  33.6 us
    psum x1, waiting for transfers between devices, shards(): lax.psum((jnp.sum(w_gate * w_gate, axis=1), jnp.sum(w_up * w_up, axis=1))...  31.5 us
    reduce_sum x1, other arithmetic, shards(): jnp.sum(w_up * w_up, axis=1)  17.3 us
    all_gather x1, blocking collectives, shards(): serve_router = lax.all_gather(row_router, 'bank', axis=1, tiled=True)  16.1 us
  transfers between devices with their start and end apart: 3, of which 2 were waited for; matrix products, arithmetic and copies ran while one was open for 17% of the time, Pallas kernels for 0%

commit v1 on v0

--- a/solution.py
+++ b/solution.py
@@ -2,6 +2,16 @@
 import jax.numpy as jnp
 from jax import lax
 from jax.sharding import PartitionSpec as P
+
+_define_target = lambda inp: jnp.concatenate(
+    lax.all_to_all(
+        jnp.stack(jnp.split(inp, lax.psum(1, axis_name="zero"), axis=2), axis=0),
+        axis_name="zero",
+        split_axis=0,
+        concat_axis=0,
+    ),
+    axis=1,
+)
 
 
 def shards(w_gate, w_up, router_weight, router_gain):
@@ -15,7 +25,7 @@
         (w_up / jnp.expand_dims(scale_up, 1)).astype(jnp.bfloat16),
     )
     serve_gate, serve_up = (
-        lax.all_to_all(narrow_gate, "zero", split_axis=2, concat_axis=1, tiled=True),
+        _define_target(narrow_gate),
         lax.all_to_all(narrow_up, "zero", split_axis=2, concat_axis=1, tiled=True),
     )
     scale_gate = lax.dynamic_slice_in_dim(

time: 483 us -> 466 us (0.965)
  local copies, waits for them, and re-layouts: 121 us -> 108 us
    all_to_all x1, waiting for transfers between devices: 0.01 us -> 99.5 us  [lax.all_to_all(jnp.stack(jnp.split(inp, lax.psum(1, axis_name='zero'), ax...]
    all_to_all x1, waiting for transfers between devices: 99.5 us -> 0.01 us  [shards(): lax.all_to_all(narrow_up, 'zero', split_axis=2, concat_axis=1, tiled=True)]
    all_to_all x2 -> x0, local copies, waits for them, and re-layouts: 33.6 us -> none  [shards(): lax.all_to_all(narrow_gate, 'zero', split_axis=2, concat_axis=1, tiled=True)]
    reshape x0 -> x1, local copies, waits for them, and re-layouts: none -> 10.9 us  [jnp.concatenate(lax.all_to_all(jnp.stack(jnp.split(inp, lax.psum(1, axis_...]
    unnamed x9 -> x16, local copies, waits for them, and re-layouts: 51.3 us -> 59.8 us
where the time goes in v1:
time: 466 us; the launch traced here: 465 us
  blocking collectives  158 us (34%)
  waiting for transfers between devices  132 us (28%)
  local copies, waits for them, and re-layouts  108 us (23%)
  other arithmetic  41.7 us (9%)
  between operations  14.1 us (3%)
  starting transfers between devices  10.8 us (2%)
    all_gather x1, blocking collectives, shards(): row_router = lax.all_gather(part_router, 'zero', axis=0, tiled=True)  142 us
    all_to_all x1, waiting for transfers between devices, lax.all_to_all(jnp.stack(jnp.split(inp, lax.psum(1, axis_name='zero'), ax...  99.5 us
    unnamed x16, local copies, waits for them, and re-layouts  59.8 us
    all_to_all x2, local copies, waits for them, and re-layouts, shards(): lax.all_to_all(narrow_up, 'zero', split_axis=2, concat_axis=1, tiled=True)  33.6 us
    psum x1, waiting for transfers between devices, shards(): lax.psum((jnp.sum(w_gate * w_gate, axis=1), jnp.sum(w_up * w_up, axis=1))...  32 us
    reduce_sum x1, other arithmetic, shards(): jnp.sum(w_up * w_up, axis=1)  17.3 us
    all_gather x1, blocking collectives, shards(): serve_router = lax.all_gather(row_router, 'bank', axis=1, tiled=True)  16.1 us
    convert_element_type x1, other arithmetic, shards(): (w_up / jnp.expand_dims(scale_up, 1)).astype(jnp.bfloat16)  14.1 us
  transfers between devices with their start and end apart: 3, of which 2 were waited for; matrix products, arithmetic and copies ran while one was open for 17% of the time, Pallas kernels for 0%

profile of v1, /device:TPU:0, one launch (start us, length us, event | category | flops | bytes accessed | tf_op | source)
XLA Modules:
  0.0 464.5 jit_solution(98903679744253797)
XLA Ops:
  7.2 17.3 %multiply_reduce_fusion = (f32[32,768]{1,0:T(8,128)}, f32[32,768]{1,0:T(8,128)}) fusion(f32[32,256,768]{2,1,0:T(8,128)} %param.5, f32[32,256,768]{2,1,0:T(8,128)} %param.4), kind=kLoop, calls=%fused_computation.1 | loop fusion | flops 25116672 | bytes 50528256 | tf_op jit(solution)/shard_map/reduce_sum | solution.py:19
  24.5 24.7 %copy.25 = f32[32,256,768]{1,2,0:T(8,128)} copy(f32[32,256,768]{2,1,0:T(8,128)} %param.4) | data formatting | bytes 50331648 | tf_op args[0]
  49.2 32.0 %all-reduce.3.cloned.1.call-done = (f32[32,768]{1,0:T(8,128)}, f32[32,768]{1,0:T(8,128)}) async-done(((f32[32,768]{1,0:T(8,128)}, f32[32,768]{1,0:T(8,128)}), (f32[32,768]{1,0:T(8,128)}, f32[32,768]{1,0:T(8,128)})) %all-reduce.3.cloned.1.call-update) | async-done | bytes 196624 | tf_op jit(solution)/shard_map/psum | solution.py:18
  81.1 0.9 sqrt.6
  82.1 10.3 %divide_convert_fusion.1 = bf16[32,256,768]{1,2,0:T(8,128)(2,1)S(1)} fusion(f32[32,256,768]{1,2,0:T(8,128)} %copy.25, f32[32,768]{1,0:T(8,128)S(1)} %sqrt.6), kind=kLoop, calls=%fused_computation.2 | loop fusion | flops 12582912 | bytes 37847040 | tf_op jit(solution)/shard_map/convert_element_type | solution.py:24
  92.3 1.3 fusion.7
  93.6 1.3 fusion.6
  94.9 1.3 fusion.5
  96.2 1.3 fusion.4
  97.5 1.3 fusion.3
  98.7 1.3 fusion.2
  100.0 1.3 fusion.1
  101.3 1.3 fusion
  102.6 5.4 %all-to-all-start = ((bf16[8,32,256,96]{2,3,1,0:T(8,128)(2,1)}), bf16[8,32,256,96]{2,3,1,0:T(8,128)(2,1)}, u32[]{:S(2)}, u32[]{:S(2)}) async-start(bf16[8,32,256,96]{2,3,1,0:T(8,128)(2,1)} %fusion), calls=%async_computation | async-start | bytes 25165824 | tf_op jit(solution)/shard_map/all_to_all | solution.py:7
  108.0 25.1 %copy.28 = f32[32,256,768]{1,0,2:T(8,128)} copy(f32[32,256,768]{2,1,0:T(8,128)} %param.5) | data formatting | bytes 50331648 | tf_op args[1]
  133.3 14.1 %divide_convert_fusion = bf16[32,256,768]{1,0,2:T(8,128)(2,1)} fusion(f32[32,256,768]{1,0,2:T(8,128)} %copy.28, f32[32,768]{0,1:T(8,128)S(1)} %copy.27), kind=kLoop, calls=%fused_computation | loop fusion | flops 12582912 | bytes 37847040 | tf_op jit(solution)/shard_map/convert_element_type | solution.py:25
  147.5 99.5 %all-to-all-done = bf16[8,32,256,96]{2,3,1,0:T(8,128)(2,1)} async-done(((bf16[8,32,256,96]{2,3,1,0:T(8,128)(2,1)}), bf16[8,32,256,96]{2,3,1,0:T(8,128)(2,1)}, u32[]{:S(2)}, u32[]{:S(2)}) %all-to-all-start) | async-done | bytes 12582944 | tf_op jit(solution)/shard_map/all_to_all | solution.py:7
  247.0 5.4 %all-to-all-start.1 = ((bf16[32,256,768]{1,0,2:T(8,128)(2,1)}), bf16[32,256,768]{1,0,2:T(8,128)(2,1)}, u32[]{:S(2)}, u32[]{:S(2)}) async-start(bf16[32,256,768]{1,0,2:T(8,128)(2,1)} %divide_convert_fusion), calls=%async_computation.1 | async-start | bytes 25165824 | tf_op jit(solution)/shard_map/all_to_all | solution.py:29
  252.4 142.4 %all_gather.6 = bf16[2048,32]{0,1:T(8,128)(2,1)S(1)} all-gather(bf16[256,32]{0,1:T(8,128)(2,1)S(1)} %multiply_convert_fusion), channel_id=1, replica_groups=mesh['bank'=4,'zero'=8] {'zero'}, dimensions={0}, use_global_device_ids=true | all-gather | bytes 147456 | tf_op jit(solution)/shard_map/all_gather | solution.py:38
  394.8 16.1 %all_gather.7 = bf16[2048,128]{0,1:T(8,128)(2,1)S(1)} all-gather(bf16[2048,32]{0,1:T(8,128)(2,1)S(1)} %all_gather.6), channel_id=1, replica_groups=mesh['bank'=4,'zero'=8] {'bank'}, dimensions={1}, use_global_device_ids=true | all-gather | bytes 655360 | tf_op jit(solution)/shard_map/all_gather | solution.py:39
  410.9 1.0 copy.31
  413.2 10.9 %copy.33 = bf16[8,32,12,8,256]{4,3,0,2,1:T(8,128)(2,1)} copy(bf16[8,32,12,8,256]{4,3,2,1,0:T(8,128)(2,1)} %bitcast.12) | data formatting | bytes 25165824 | tf_op jit(solution)/shard_map/reshape | solution.py:6
  424.1 14.1 %copy.30 = bf16[32,8,256,96]{2,1,3,0:T(8,128)(2,1)} copy(bf16[32,8,256,96]{2,0,3,1:T(8,128)(2,1)} %bitcast.11) | data formatting | bytes 25165824 | tf_op jit(solution)/shard_map/all_to_all | solution.py:29
  438.2 19.5 %all_to_all.20 = bf16[32,2048,96]{1,2,0:T(8,128)(2,1)} reshape(bf16[32,8,256,96]{2,1,3,0:T(8,128)(2,1)} %copy.30) | data formatting | bytes 25165824 | tf_op jit(solution)/shard_map/all_to_all | solution.py:29
  (14 shorter events, 1.6 us)
Async XLA Ops:
  7.2 74.0 %all-reduce.3.cloned.1.call-start = ((), (), s32[]{:S(2)}) async-start(), calls=%async_computation.2 | async-start | bytes 393216 | tf_op jit(solution)/shard_map/psum | solution.py:18
  102.6 144.4 %all-to-all-start = ((bf16[8,32,256,96]{2,3,1,0:T(8,128)(2,1)}), bf16[8,32,256,96]{2,3,1,0:T(8,128)(2,1)}, u32[]{:S(2)}, u32[]{:S(2)}) async-start(bf16[8,32,256,96]{2,3,1,0:T(8,128)(2,1)} %fusion), calls=%async_computation | async-start | bytes 25165824 | tf_op jit(solution)/shard_map/all_to_all | solution.py:7
  108.0 25.1 %copy-start = (f32[32,768]{1,0:T(8,128)S(1)}, f32[32,768]{1,0:T(8,128)}, u32[]{:S(2)}) copy-start(f32[32,768]{1,0:T(8,128)} %get-tuple-element.16) | copy-start | bytes 294916
  147.5 104.9 %copy-start.1 = (f32[256,32]{0,1:T(8,128)S(1)}, f32[256,32]{0,1:T(8,128)}, u32[]{:S(2)}) copy-start(f32[256,32]{0,1:T(8,128)} %param.6) | copy-start | bytes 98308
  147.5 104.9 %copy-start.2 = (f32[256]{0:T(256)S(1)}, f32[256]{0:T(256)}, u32[]{:S(2)}) copy-start(f32[256]{0:T(256)} %param.7) | copy-start | bytes 3076
  247.0 177.1 %all-to-all-start.1 = ((bf16[32,256,768]{1,0,2:T(8,128)(2,1)}), bf16[32,256,768]{1,0,2:T(8,128)(2,1)}, u32[]{:S(2)}, u32[]{:S(2)}) async-start(bf16[32,256,768]{1,0,2:T(8,128)(2,1)} %divide_convert_fusion), calls=%async_computation.1 | async-start | bytes 25165824 | tf_op jit(solution)/shard_map/all_to_all | solution.py:29
Sparse Core Ops, SparseCore 0:
  24.6 56.4 all-reduce.2
